TPU v7x, 32 devices: a 4x4x1 block of a 4x4x8 slice. The times are simulated.
32 devices in a mesh: dp: 1 (over z), fsdp: 32 (over y, x, core).
Axes of the slice: x: 4, y: 4, z: 1, core: 2. Of those that a mesh axis runs over, the one named last changes fastest.
The devices are a block of a 4x4x8 slice.
Arguments:
- prompts: bfloat16 [512, 128, 2560], P(('dp', 'fsdp'))
- ln1_gain: bfloat16 [2560], P('fsdp')
- ln1_bias: bfloat16 [2560], P('fsdp')
- w_qkv: bfloat16 [2560, 3, 32, 80], P('fsdp')
- b_qkv: bfloat16 [7680], P('fsdp')
- w_out: bfloat16 [2560, 2560], P('fsdp')
- b_out: bfloat16 [2560], P('fsdp')
- ln2_gain: bfloat16 [2560], P('fsdp')
- ln2_bias: bfloat16 [2560], P('fsdp')
- w_up: bfloat16 [2560, 10240], P('fsdp')
- b_up: bfloat16 [10240], P('fsdp')
- w_down: bfloat16 [10240, 2560], P('fsdp')
- b_down: bfloat16 [2560], P('fsdp')
Outputs:
- output 1: bfloat16 [512, 128, 2560], P(('dp', 'fsdp'))
- output 2: bfloat16 [512, 128, 32, 80], P(('dp', 'fsdp'))
- output 3: bfloat16 [512, 128, 32, 80], P(('dp', 'fsdp'))
All inputs are finite; a program needn't handle non-finite values.
Results may differ from a plain program's by a relative error of at most 0.00904977.
Values are sent between devices in bfloat16 or wider.
A program may use at most 768 MiB of HBM per device.

v0:
```python
import jax
import jax.numpy as jnp
from jax import lax
from jax.sharding import PartitionSpec as P

LN_EPS = 1e-5
QUERY_BLOCK = 256


def layer_norm(act, gain, shift):
    act_f32 = act.astype(jnp.float32)
    mean_val = jnp.mean(act_f32, axis=-1, keepdims=True)
    centered = act_f32 - mean_val
    var_val = jnp.mean(centered * centered, axis=-1, keepdims=True)
    normed = centered * lax.rsqrt(var_val + LN_EPS)
    return (normed * gain.astype(jnp.float32) + shift.astype(jnp.float32)).astype(jnp.bfloat16)


def causal_attention(queries, keys, values):
    seq_len = queries.shape[1]
    q_block = min(seq_len, QUERY_BLOCK)
    scale = queries.shape[-1] ** -0.5
    key_pos = jnp.arange(seq_len)

    def one_block(blk_idx):
        start = blk_idx * q_block
        q_blk = lax.dynamic_slice_in_dim(queries, start, q_block, axis=1)
        scores = jnp.einsum('bqhe,bkhe->bhqk', q_blk, keys, preferred_element_type=jnp.float32) * scale
        allowed = key_pos[None, :] <= (start + jnp.arange(q_block))[:, None]
        scores = jnp.where(allowed, scores, -jnp.inf)
        probs = jax.nn.softmax(scores, axis=-1).astype(jnp.bfloat16)
        return jnp.einsum('bhqk,bkhe->bqhe', probs, values, preferred_element_type=jnp.float32).astype(jnp.bfloat16)

    return lax.map(one_block, jnp.arange(seq_len // q_block))


def solution(mesh):
    batch_axes = ('dp', 'fsdp')

    def gather_full(shard):
        return lax.all_gather(shard, 'fsdp', axis=0, tiled=True)

    def local_layer(prompts, ln1_gain, ln1_bias, w_qkv, b_qkv, w_out, b_out, ln2_gain, ln2_bias, w_up, b_up, w_down, b_down):
        batch_loc, seq_len, d_model = prompts.shape
        heads, head_dim = w_qkv.shape[2], w_qkv.shape[3]
        normed1 = layer_norm(prompts, gather_full(ln1_gain), gather_full(ln1_bias))
        w_qkv_full = gather_full(w_qkv)
        b_qkv_full = gather_full(b_qkv)
        proj_qkv = jnp.einsum('bsd,djhe->jbshe', normed1, w_qkv_full, preferred_element_type=jnp.float32)
        proj_qkv = (proj_qkv + b_qkv_full.astype(jnp.float32).reshape(3, 1, 1, heads, head_dim)).astype(jnp.bfloat16)
        ctx_blocks = causal_attention(proj_qkv[0], proj_qkv[1], proj_qkv[2])
        w_out_full = gather_full(w_out).reshape(heads, head_dim, d_model)
        b_out_full = gather_full(b_out)
        attn_out = jnp.einsum('nbqhe,hec->bnqc', ctx_blocks, w_out_full, preferred_element_type=jnp.float32).reshape(batch_loc, seq_len, d_model)
        resid = (prompts.astype(jnp.float32) + attn_out + b_out_full.astype(jnp.float32)).astype(jnp.bfloat16)
        normed2 = layer_norm(resid, gather_full(ln2_gain), gather_full(ln2_bias))
        w_up_full = gather_full(w_up)
        b_up_full = gather_full(b_up)
        hidden = jnp.einsum('bsd,df->bsf', normed2, w_up_full, preferred_element_type=jnp.float32) + b_up_full.astype(jnp.float32)
        hidden = jax.nn.gelu(hidden, approximate=True).astype(jnp.bfloat16)
        w_down_full = gather_full(w_down)
        b_down_full = gather_full(b_down)
        mlp_out = jnp.einsum('bsf,fd->bsd', hidden, w_down_full, preferred_element_type=jnp.float32)
        layer_out = (resid.astype(jnp.float32) + mlp_out + b_down_full.astype(jnp.float32)).astype(jnp.bfloat16)
        return layer_out, proj_qkv[1], proj_qkv[2]

    weight_spec = P('fsdp')
    return jax.shard_map(local_layer, mesh=mesh, in_specs=(P(batch_axes),) + (weight_spec,) * 12, out_specs=(P(batch_axes), P(batch_axes), P(batch_axes)), check_vma=False)
```

profile of v0, /device:TPU:97, one launch (start us, length us, event | category | flops | bytes accessed | tf_op | source)
XLA Modules:
  0.0 880.4 jit_solution(15195304332126432349)
XLA Ops:
  7.2 0.1 all-reduce.11.cloned.1.call-start
  7.3 0.9 dynamic-update-slice
  8.1 0.0 copy-start.5
  8.1 0.9 dynamic-update-slice.1
  9.0 0.0 copy-start.6
  9.0 0.9 dynamic-update-slice.3
  9.8 0.9 dynamic-update-slice.4
  10.7 0.9 dynamic-update-slice.5
  11.6 0.9 dynamic-update-slice.7
  12.4 0.9 dynamic-update-slice.6
  13.3 0.9 dynamic-update-slice.2
  14.2 0.0 copy-done.5
  14.2 0.0 copy-done.6
  14.2 0.0 copy-done.7
  14.2 0.0 copy-done.8
  14.2 0.0 copy-done.9
  14.2 0.0 copy-done.4
  14.2 0.0 copy-done.1
  14.2 0.5 copy-done.2
  14.8 0.1 all-reduce.11.cloned.1.call-update
  14.8 0.1 all-gather.5.cloned.1.call-start
  14.9 0.7 all-gather.5.cloned.1.call-update
  15.6 0.1 all-gather.7.cloned.1.call-start
  15.7 0.7 all-gather.7.cloned.1.call-update
  16.4 0.1 all-gather.9.cloned.1.call-start
  16.5 0.6 all-gather.9.cloned.1.call-update
  17.1 0.1 all-gather.11.cloned.1.call-start
  17.1 0.6 all-gather.11.cloned.1.call-update
  17.7 0.6 iota_compare_fusion
  18.3 5.4 convert_reduce_fusion.1
  23.8 6.8 fusion.32
  30.6 81.2 %all-reduce.11.cloned.1.call-done = (bf16[2560]{0:T(1024)(128)(2,1)}, bf16[7680]{0:T(1024)(128)(2,1)}, bf16[2560]{0:T(1024)(128)(2,1)}, bf16[2560]{0:T(1024)(128...) async-done(((bf16[2560]{0:T(1024)(128)(2,1)}, bf16[7680]{0:T(1024)(128)(2,1)}, ...) | async-done | bytes 66576
  111.8 0.8 reshape.50
  112.6 0.7 convert_element_type.63
  113.3 0.7 convert_element_type.64
  114.0 1.3 convert_element_type.71
  115.3 1.3 convert_element_type.74
  116.6 1.3 convert_element_type.75
  117.9 1.3 convert_element_type.77
  119.2 1.3 convert_element_type.79
  120.5 178.2 %all-gather.5.cloned.1.call-done = bf16[2560,3,32,80]{3,2,1,0:T(8,128)(2,1)} async-done(((bf16[80,3,32,80]{3,2,1,0:T(8,128)(2,1)}), bf16[2560,3,32,80]{3,2,1,0:T(8,128)(2,1)}) %all-gather.5.cloned.1.call-update) | async-done | bytes 39321616 | tf_op jit(solution)/shard_map/all_gather | solution.py:41
  298.7 72.5 %copy.17 = bf16[2560,3,32,80]{0,3,2,1:T(8,128)(2,1)} copy(bf16[2560,3,32,80]{3,2,1,0:T(8,128)(2,1)} %all-gather.5.cloned.1.call-done) | data formatting | bytes 78643200 | tf_op jit(solution)/shard_map/all_gather | solution.py:41
  371.3 94.4 %fusion.20 = bf16[3,16,128,32,80]{2,4,3,0,1:T(8,128)(2,1)} fusion(f32[3,32,80]{2,1,0:T(8,128)S(1)} %reshape.50, bf16[2560,3,32,80]{0,3,2,1:T(8,128)(2,1)} %copy.17, bf16[16,128,2560]{2,1,0:T(8,128)(2,1)} %param.13, f32[2560]{0:T(1024)S(1)} %convert_element_type.64, f32[2560]{0:T(1024)S(1)} %convert_element_type.63, f32[16,128]{1,0:T(8,128)S(1)} %add_rsqrt_fusion.1, ...), kind=kOutput, calls=%fused_computation.24 | convolution fusion | flops 80593551360 | bytes 81332224 | tf_op jit(solution)/shard_map/bsd,djhe->jbshe/dot_general | solution.py:49
  465.7 18.2 %slice_bitcast_fusion = (bf16[16,128,32,80]{1,3,2,0:T(8,128)(2,1)}, bf16[16,128,32,80]{1,3,2,0:T(8,128)(2,1)}) fusion(bf16[3,16,128,32,80]{2,4,3,0,1:T(8,128)(2,1)} %fusion.20), kind=kLoop, calls=%fused_computation.53 | loop fusion | bytes 41943040 | tf_op jit(solution)/shard_map/squeeze | solution.py:51
  483.9 18.1 %fusion.47 = f32[16,32,128,128]{2,3,1,0:T(8,128)} fusion(bf16[16,128,32,80]{1,3,2,0:T(8,128)(2,1)} %get-tuple-element.29, bf16[3,16,128,32,80]{2,4,3,0,1:T(8,128)(2,1)} %fusion.20), kind=kOutput, calls=%fused_computation.55 | convolution fusion | flops 1342177280 | bytes 54525952 | tf_op jit(solution)/shard_map/while/body/eval_jaxpr/bqhe,bkhe->bhqk/dot_general | solution.py:28
  501.9 0.0 copy-done.10
  501.9 38.3 %fusion.71 = (f32[16,32,128]{2,1,0:T(8,128)S(1)}, f32[16,32,128,128]{2,3,1,0:T(8,128)}) fusion(f32[16,32,128,128]{2,3,1,0:T(8,128)} %fusion.47, pred[128,128]{0,1:T(8,128)(4,1)S(1)} %copy-done.10), kind=kOutput, calls=%fused_computation.79 | output fusion | flops 50331776 | bytes 67387392 | tf_op jit(solution)/shard_map/while/body/eval_jaxpr/sub | solution.py:31
  540.3 20.2 %fusion.64.clone.4 = bf16[16,128,32,80]{1,3,2,0:T(8,128)(2,1)} fusion(bf16[16,128,32,80]{1,3,2,0:T(8,128)(2,1)} %get-tuple-element.30, f32[16,32,128,128]{2,3,1,0:T(8,128)} %get-tuple-element.32, f32[16,32,128]{2,1,0:T(8,128)S(1)} %get-tuple-element.31), kind=kOutput, calls=%fused_computation.58.clone.clone.clone.clone.clone.1 | convolution fusion | flops 1364197376 | bytes 54788096 | tf_op jit(solution)/shard_map/while/body/eval_jaxpr/bhqk,bkhe->bqhe/dot_general | solution.py:32
  560.4 0.0 copy-done.14
  560.4 0.0 copy-start.13
  560.4 35.3 %convert_reduce_fusion = (f32[16,128]{1,0:T(8,128)S(1)}, bf16[16,128,2560]{2,1,0:T(8,128)(2,1)S(1)}) fusion(f32[2560]{0:T(1024)S(1)} %copy-done.14, bf16[32,80,2560,1]{2,1,0,3:T(8,128)(2,1)} %bitcast.57, bf16[16,128,2560]{2,1,0:T(8,128)(2,1)} %param.13, bf16[16,128,32,80]{1,3,2,0:T(8,128)(2,1)} %fusion.64.clone.4), kind=kOutput, calls=%fused_computation.27 | convolution fusion | flops 26875000832 | bytes 44582912 | tf_op jit(solution)/shard_map/nbqhe,hec->bnqc/dot_general | solution.py:54
  595.7 0.0 copy-start
  595.8 4.1 copy-done
  599.8 2.9 fusion.28
  602.7 0.0 all-gather.9.cloned.1.call-done
  602.7 0.0 copy-done.12
  602.7 0.0 copy-done.13
  602.8 0.0 copy-start.3
  602.8 0.0 copy-start.11
  602.8 132.9 %fusion.11 = f32[16,128,10240]{2,1,0:T(8,128)} fusion(bf16[2560,10240]{1,0:T(8,128)(2,1)} %all-gather.9.cloned.1.call-done, bf16[16,128,2560]{2,1,0:T(8,128)(2,1)} %copy-done, f32[2560]{0:T(1024)S(1)} %copy-done.13, f32[2560]{0:T(1024)S(1)} %copy-done.12, f32[16,128]{1,0:T(8,128)S(1)} %add_rsqrt_fusion, f32[16,128]{1,0:T(8,128)S(1)} %broadcast_multiply_fusion), kind=kOutput, calls=%fused_computation.13 | convolution fusion | flops 107405639680 | bytes 146837504 | tf_op jit(solution)/shard_map/bsd,df->bsf/dot_general | solution.py:59
  735.7 0.0 all-gather.11.cloned.1.call-done
  735.7 0.0 copy-done.3
  735.7 0.0 copy-done.11
  735.7 137.9 %fusion.39 = bf16[16,128,2560]{2,1,0:T(8,128)(2,1)} fusion(bf16[16,128,2560]{2,1,0:T(8,128)(2,1)} %copy-done, f32[2560]{0:T(1024)S(1)} %copy-done.11, bf16[10240,2560]{1,0:T(8,128)(2,1)} %all-gather.11.cloned.1.call-done, f32[16,128,10240]{2,1,0:T(8,128)} %fusion.11, f32[10240]{0:T(1024)S(1)} %copy-done.3), kind=kOutput, calls=%fused_computation.47 | convolution fusion | flops 107604869120 | bytes 157337600 | tf_op jit(solution)/shard_map/bsf,fd->bsd/dot_general | solution.py:63
  (22 shorter events, 0.1 us)
Async XLA Ops:
  7.2 104.6 %all-reduce.11.cloned.1.call-start = ((), (), s32[]{:S(2)}) async-start(), calls=%async_computation.4 | async-start | bytes 147456
  8.1 6.0 copy-start.5
  9.0 5.2 copy-start.6
  9.8 4.3 copy-start.7
  10.7 3.5 copy-start.8
  11.6 2.6 copy-start.9
  12.4 1.8 copy-start.4
  13.3 0.9 copy-start.1
  14.2 0.6 copy-start.2
  14.8 283.9 %all-gather.5.cloned.1.call-start = ((), (), s32[]{:S(2)}) async-start(), calls=%async_computation | async-start | bytes 64880640 | tf_op jit(solution)/shard_map/all_gather | solution.py:41
  15.6 544.8 %all-gather.7.cloned.1.call-start = ((), (), s32[]{:S(2)}) async-start(), calls=%async_computation.1 | async-start | bytes 13516800 | tf_op jit(solution)/shard_map/all_gather | solution.py:41
  16.4 586.3 %all-gather.9.cloned.1.call-start = ((), (), s32[]{:S(2)}) async-start(), calls=%async_computation.2 | async-start | bytes 54067200 | tf_op jit(solution)/shard_map/all_gather | solution.py:41
  17.1 718.6 %all-gather.11.cloned.1.call-start = ((), (), s32[]{:S(2)}) async-start(), calls=%async_computation.3 | async-start | bytes 54067200 | tf_op jit(solution)/shard_map/all_gather | solution.py:41
  483.9 18.1 %copy-start.10 = (pred[128,128]{0,1:T(8,128)(4,1)S(1)}, pred[128,128]{0,1:T(8,128)(4,1)}, u32[]{:S(2)}) copy-start(pred[128,128]{0,1:T(8,128)(4,1)} %iota_compare_fusion) | copy-start | bytes 49156
  540.2 20.2 %copy-start.14 = (f32[2560]{0:T(1024)S(1)}, f32[2560]{0:T(1024)}, u32[]{:S(2)}) copy-start(f32[2560]{0:T(1024)} %convert_element_type.71) | copy-start | bytes 30724
  560.4 42.3 %copy-start.12 = (f32[2560]{0:T(1024)S(1)}, f32[2560]{0:T(1024)}, u32[]{:S(2)}) copy-start(f32[2560]{0:T(1024)} %convert_element_type.74) | copy-start | bytes 30724
  560.4 42.3 %copy-start.13 = (f32[2560]{0:T(1024)S(1)}, f32[2560]{0:T(1024)}, u32[]{:S(2)}) copy-start(f32[2560]{0:T(1024)} %convert_element_type.75) | copy-start | bytes 30724
  595.7 4.1 copy-start
  602.8 133.0 %copy-start.3 = (f32[10240]{0:T(1024)S(1)}, f32[10240]{0:T(1024)}, u32[]{:S(2)}) copy-start(f32[10240]{0:T(1024)} %convert_element_type.77) | copy-start | bytes 122884
  602.8 133.0 %copy-start.11 = (f32[2560]{0:T(1024)S(1)}, f32[2560]{0:T(1024)}, u32[]{:S(2)}) copy-start(f32[2560]{0:T(1024)} %convert_element_type.79) | copy-start | bytes 30724
Sparse Core Ops, SparseCore 0:
  15.0 96.8 all-reduce.10
  113.9 184.7 all-gather.4
  300.8 57.5 all-gather.6
  360.3 157.1 all-gather.8
  519.4 156.6 all-gather.10
where the time goes:
time: 888 us; the launch traced here: 880 us
  matrix products  439 us (49%)
  waiting for transfers between devices  262 us (30%)
  local copies, waits for them, and re-layouts  103 us (12%)
  other arithmetic  61.9 us (7%)
  between operations  14.3 us (2%)
    all_gather x4, waiting for transfers between devices, gather_full(): return lax.all_gather(shard, 'fsdp', axis=0, tiled=True)  178 us
    dot_general x1, matrix products, local_layer(): jnp.einsum('bsf,fd->bsd', hidden, w_down_full, preferred_element_type=jnp...  138 us
    dot_general x1, matrix products, local_layer(): jnp.einsum('bsd,df->bsf', normed2, w_up_full, preferred_element_type=jnp....  133 us
    dot_general x1, matrix products, local_layer(): jnp.einsum('bsd,djhe->jbshe', normed1, w_qkv_full, preferred_element_type...  94.4 us
    unnamed x6, waiting for transfers between devices  83.8 us
    all_gather x1, local copies, waits for them, and re-layouts, gather_full(): return lax.all_gather(shard, 'fsdp', axis=0, tiled=True)  72.5 us
    sub x1, other arithmetic, one_block(): probs = jax.nn.softmax(scores, axis=-1).astype(jnp.bfloat16)  38.3 us
    dot_general x1, matrix products, local_layer(): jnp.einsum('nbqhe,hec->bnqc', ctx_blocks, w_out_full, preferred_element_t...  35.3 us
  transfers between devices with their start and end apart: 5, of which 2 were waited for; matrix products, arithmetic and copies ran while one was open for 52% of the time, Pallas kernels for 0%

commit v1 on v0

v1 whole, which is shorter than its diff:
```python
import functools

import jax
import jax.numpy as jnp
from jax import lax
from jax.experimental import pallas as pl
from jax.experimental.pallas import tpu as pltpu
from jax.sharding import PartitionSpec as P

LN_EPS = 1e-5
LANES = 128
F32 = jnp.float32
BF16 = jnp.bfloat16


def layer_norm(act, gain, shift):
    act_f32 = act.astype(F32)
    mean_val = jnp.mean(act_f32, axis=-1, keepdims=True)
    centered = act_f32 - mean_val
    var_val = jnp.mean(centered * centered, axis=-1, keepdims=True)
    normed = centered * lax.rsqrt(var_val + LN_EPS)
    return (normed * gain + shift).astype(BF16)


def params(limit_mib, axes):
    return pltpu.CompilerParams(
        dimension_semantics=("arbitrary",) * axes, vmem_limit_bytes=limit_mib << 20
    )


def cost(flops, nbytes):
    return pl.CostEstimate(flops=int(flops), bytes_accessed=int(nbytes), transcendentals=0)


def row_chunks(rows, size):
    return [(start, min(size, rows - start)) for start in range(0, rows, size)]


def proj_kernel(epilogue, chunk, x_ref, w_ref, b_ref, o_ref):
    for start, size in row_chunks(x_ref.shape[0], chunk):
        acc = jnp.dot(x_ref[start:start + size, :], w_ref[...], preferred_element_type=F32)
        o_ref[start:start + size, :] = epilogue(acc + b_ref[...]).astype(o_ref.dtype)


def project(x, w, first_col, n_cols, bias, epilogue, bm, bn, chunk=256):
    rows, k = x.shape
    off = first_col // bn
    return pl.pallas_call(
        functools.partial(proj_kernel, epilogue, chunk),
        out_shape=jax.ShapeDtypeStruct((rows, n_cols), BF16),
        grid=(rows // bm, n_cols // bn),
        in_specs=[
            pl.BlockSpec((bm, k), lambda m, n: (m, 0)),
            pl.BlockSpec((k, bn), lambda m, n: (0, n + off)),
            pl.BlockSpec((1, bn), lambda m, n: (0, n)),
        ],
        out_specs=pl.BlockSpec((bm, bn), lambda m, n: (m, n)),
        compiler_params=params(58, 2),
        cost_estimate=cost(2 * rows * k * n_cols, 2 * (rows * k + k * n_cols + rows * n_cols)),
    )(x, w, bias)


def kv_kernel(half, bn, seq, chunk, x_ref, w_ref, b_ref, k_hbm, v_hbm, buf, sem):
    n = pl.program_id(0)
    total = 2 * half
    slot = lax.rem(n, 2)

    def copy(dst, col_block, which):
        cols = pl.ds(pl.multiple_of(col_block * bn, bn), bn)
        return pltpu.make_async_copy(buf.at[which], dst.at[:, cols, :], sem.at[which])

    @pl.when(n >= 2)
    def _():
        copy(k_hbm, 0, slot).wait()

    for start, size in row_chunks(x_ref.shape[0], chunk):
        acc = jnp.dot(x_ref[start:start + size, :], w_ref[...], preferred_element_type=F32)
        turned = (acc + b_ref[...]).astype(BF16).T
        for i in range(size // seq):
            buf[slot, start // seq + i] = turned[:, i * seq:(i + 1) * seq]

    @pl.when(n < half)
    def _():
        copy(k_hbm, n, slot).start()

    @pl.when(n >= half)
    def _():
        copy(v_hbm, n - half, slot).start()

    @pl.when(n == total - 1)
    def _():
        copy(v_hbm, 0, 1 - slot).wait()
        copy(v_hbm, 0, slot).wait()


def keys_values(x, w, first_col, width, bias, seq, bn=256, chunk=256):
    rows, k = x.shape
    batch = rows // seq
    off, half = first_col // bn, width // bn
    shape = jax.ShapeDtypeStruct((batch, width, seq), BF16)
    return pl.pallas_call(
        functools.partial(kv_kernel, half, bn, seq, chunk),
        out_shape=(shape, shape),
        grid=(2 * half,),
        in_specs=[
            pl.BlockSpec((rows, k), lambda n: (0, 0), pipeline_mode=pl.Buffered(1)),
            pl.BlockSpec((k, bn), lambda n: (0, n + off)),
            pl.BlockSpec((1, bn), lambda n: (0, n)),
        ],
        out_specs=(pl.BlockSpec(memory_space=pl.ANY), pl.BlockSpec(memory_space=pl.ANY)),
        scratch_shapes=[pltpu.VMEM((2, batch, bn, seq), BF16), pltpu.SemaphoreType.DMA((2,))],
        compiler_params=params(58, 1),
        cost_estimate=cost(4 * rows * k * width, 2 * (rows * k + 2 * k * width + 2 * rows * width)),
    )(x, w, bias)


def attn_kernel(heads, head_dim, q_ref, k_ref, v_ref, o_ref):
    seq = q_ref.shape[0]
    scale = head_dim ** -0.5
    query = lax.broadcasted_iota(jnp.int32, (seq, seq), 0)
    key = lax.broadcasted_iota(jnp.int32, (seq, seq), 1)
    allowed = key <= query
    columns = {}
    for h in range(heads):
        lo, hi = h * head_dim, (h + 1) * head_dim
        base = lo // LANES * LANES
        width = pl.cdiv(hi - base, LANES) * LANES

        def padded(ref):
            parts = [ref[0, lo:hi, :]]
            if lo > base:
                parts.insert(0, jnp.zeros((lo - base, seq), BF16))
            if base + width > hi:
                parts.append(jnp.zeros((base + width - hi, seq), BF16))
            return jnp.concatenate(parts, axis=0) if len(parts) > 1 else parts[0]

        scores = jnp.dot(q_ref[:, base:base + width], padded(k_ref), preferred_element_type=F32) * scale
        scores = jnp.where(allowed, scores, -jnp.inf)
        peak = jnp.max(scores, axis=-1, keepdims=True)
        weights = jnp.exp(scores - peak)
        probs = (weights * (1.0 / jnp.sum(weights, axis=-1, keepdims=True))).astype(BF16)
        part = lax.dot_general(probs, padded(v_ref), (((1,), (1,)), ((), ())), preferred_element_type=F32)
        for i in range(width // LANES):
            col = base // LANES + i
            piece = part[:, i * LANES:(i + 1) * LANES]
            columns[col] = columns[col] + piece if col in columns else piece
        for col in [c for c in columns if (c + 1) * LANES <= hi]:
            o_ref[:, col * LANES:(col + 1) * LANES] = columns.pop(col).astype(BF16)


def attention(q, k_t, v_t, heads, head_dim):
    batch, width, seq = k_t.shape
    side = pl.BlockSpec((1, width, seq), lambda b: (b, 0, 0))
    flat = pl.BlockSpec((seq, width), lambda b: (b, 0))
    return pl.pallas_call(
        functools.partial(attn_kernel, heads, head_dim),
        out_shape=jax.ShapeDtypeStruct((batch * seq, width), BF16),
        grid=(batch,),
        in_specs=[flat, side, side],
        out_specs=flat,
        compiler_params=params(48, 1),
        cost_estimate=cost(12 * batch * heads * seq * seq * LANES, 8 * batch * seq * width),
    )(q, k_t, v_t)


def sum_kernel(n_terms, chunk, *refs):
    xs, ws = refs[:n_terms], refs[n_terms:2 * n_terms]
    base_ref, b_ref, o_ref = refs[2 * n_terms:]
    for start, size in row_chunks(o_ref.shape[0], chunk):
        acc = base_ref[start:start + size, :].astype(F32)
        for x_ref, w_ref in zip(xs, ws):
            acc = acc + jnp.dot(x_ref[start:start + size, :], w_ref[...], preferred_element_type=F32)
        if b_ref is not None:
            acc = acc + b_ref[...]
        o_ref[start:start + size, :] = acc.astype(o_ref.dtype)


def add_products(terms, base, bias, out_dtype, bm, bn, chunk=256):
    rows, cols = base.shape
    k = terms[0][2].shape[0]
    n_terms = len(terms)
    kernel = functools.partial(sum_kernel, n_terms, chunk)
    specs = [pl.BlockSpec((bm, k), functools.partial(lambda o, m, n: (m, o), xc // k)) for _, xc, _, _ in terms]
    specs += [pl.BlockSpec((k, bn), functools.partial(lambda o, m, n: (0, n + o), wc // bn)) for _, _, _, wc in terms]
    specs.append(pl.BlockSpec((bm, bn), lambda m, n: (m, n)))
    args = [t[0] for t in terms] + [t[2] for t in terms] + [base]
    if bias is not None:
        specs.append(pl.BlockSpec((1, bn), lambda m, n: (0, n)))
        args.append(bias)
        body = kernel
    else:
        def body(*refs):
            kernel(*refs[:-1], None, refs[-1])
    return pl.pallas_call(
        body,
        out_shape=jax.ShapeDtypeStruct((rows, cols), out_dtype),
        grid=(rows // bm, cols // bn),
        in_specs=specs,
        out_specs=pl.BlockSpec((bm, bn), lambda m, n: (m, n)),
        compiler_params=params(58, 2),
        cost_estimate=cost(2 * n_terms * rows * k * cols, 2 * n_terms * (rows * k + k * cols) + 6 * rows * cols),
    )(*args)


def solution(mesh):
    batch_axes = ('dp', 'fsdp')
    n_dev = mesh.shape['fsdp']

    def gather_full(shard):
        return lax.all_gather(shard, 'fsdp', axis=0, tiled=True)

    def local_layer(prompts, ln1_gain, ln1_bias, w_qkv, b_qkv, w_out, b_out, ln2_gain, ln2_bias, w_up, b_up, w_down, b_down):
        batch, seq, d = prompts.shape
        heads, head_dim = w_qkv.shape[2], w_qkv.shape[3]
        width = heads * head_dim
        own = w_out.shape[0]
        n_slabs = w_up.shape[1] // d
        rows = batch * seq

        small = jnp.concatenate(
            [v.reshape(-1, own) for v in (ln1_gain, ln1_bias, b_out, ln2_gain, ln2_bias, b_down, b_qkv, b_up)], axis=0)
        n_small = small.shape[0]
        small = jnp.pad(small, ((0, -n_small % 16), (0, -own % LANES)))
        up_slabs = w_up.reshape(own, n_dev, n_slabs, own).transpose(0, 2, 1, 3).reshape(own, n_slabs * d)
        down_slabs = [w_down[u * own:(u + 1) * own] for u in range(n_slabs)]

        cut = (n_slabs - 1) * d
        full_a = gather_full(w_qkv.reshape(own, 3 * width))
        vectors = lax.all_gather(small, 'fsdp', axis=0, tiled=False)[:, :n_small, :own].astype(F32)
        full_b = gather_full(jnp.concatenate([w_out, up_slabs[:, :cut]], axis=1))
        full_c = gather_full(jnp.concatenate([up_slabs[:, cut:], down_slabs[0], down_slabs[1]], axis=1))
        full_d = gather_full(jnp.concatenate(down_slabs[2:], axis=1))

        bqkv = vectors[:, 6:9].reshape(1, 3 * width)
        vectors = vectors.transpose(1, 0, 2).reshape(n_small, d)
        g1, s1, bo, g2, s2, bd = vectors[0], vectors[1], vectors[2:3], vectors[3], vectors[4], vectors[5:6]
        bup = vectors[9:].reshape(1, n_slabs * d)

        x = prompts.reshape(rows, d)
        normed1 = layer_norm(x, g1, s1)
        identity = lambda t: t
        gelu = functools.partial(jax.nn.gelu, approximate=True)
        k_t, v_t = keys_values(normed1, full_a, width, width, bqkv[:, width:], seq)
        q = project(normed1, full_a, 0, width, bqkv[:, :width], identity, rows // 2, 512)
        ctx = attention(q, k_t, v_t, heads, head_dim)
        x1 = add_products([(ctx, 0, full_b, 0)], x, bo, BF16, rows // 2, 512)
        normed2 = layer_norm(x1, g2, s2)
        hid_a = project(normed2, full_b, width, cut, bup[:, :cut], gelu, rows // 2, 512)
        normed2, hid_a = lax.optimization_barrier((normed2, hid_a))
        hid_b = project(normed2, full_c, 0, d, bup[:, cut:], gelu, rows // 2, 512)
        part = add_products([(hid_a, 0, full_c, d), (hid_a, d, full_c, 2 * d)], x1, bd, F32, rows // 2, 256)
        y = add_products([(hid_a, 2 * d, full_d, 0), (hid_b, 0, full_d, d)], part, None, BF16, rows // 2, 256)

        def cache(t):
            return t.reshape(batch, heads, head_dim, seq).transpose(0, 3, 1, 2)

        return y.reshape(batch, seq, d), cache(k_t), cache(v_t)

    weight_spec = P('fsdp')
    return jax.shard_map(local_layer, mesh=mesh, in_specs=(P(batch_axes),) + (weight_spec,) * 12, out_specs=(P(batch_axes), P(batch_axes), P(batch_axes)), check_vma=False)
```

time: 888 us -> 656 us (0.74)
  Pallas kernels: 0 us -> 484 us
  matrix products: 439 us -> 0 us
  waiting for transfers between devices: 262 us -> 46.5 us
  local copies, waits for them, and re-layouts: 103 us -> 31.5 us
  blocking collectives: 0 us -> 33.6 us
  other arithmetic: 61.9 us -> 38.2 us
    pallas_call x0 -> x8, Pallas kernels: none -> 484 us  [the longest x3 173 us: project(): pl.pallas_call(functools.partial(proj_kernel, epilogue, chunk), out_shape...]
    dot_general x6 -> x0, matrix products: 439 us -> none  [the longest x1 138 us: local_layer(): jnp.einsum('bsf,fd->bsd', hidden, w_down_full, preferred_element_type=jnp...]
    all_gather x4, waiting for transfers between devices: 178 us -> 46.3 us  [gather_full(): return lax.all_gather(shard, 'fsdp', axis=0, tiled=True)]
    unnamed x6 -> x4, waiting for transfers between devices: 83.8 us -> 0.21 us
    all_gather x1 -> x0, local copies, waits for them, and re-layouts: 72.5 us -> none  [gather_full(): return lax.all_gather(shard, 'fsdp', axis=0, tiled=True)]
    sub x1 -> x0, other arithmetic: 38.3 us -> none  [one_block(): probs = jax.nn.softmax(scores, axis=-1).astype(jnp.bfloat16)]
    all_gather x0 -> x1, blocking collectives: none -> 33.6 us  [local_layer(): lax.all_gather(small, 'fsdp', axis=0, tiled=False)[:, :n_small, :own]]
    reshape x0 -> x8, local copies, waits for them, and re-layouts: none -> 22.6 us  [the longest x3 17.3 us: local_layer(): w_up.reshape(own, n_dev, n_slabs, own).transpose(0, 2, 1, 3)]
  transfers between devices with their start and end apart: 5 -> 4, of which waited for: 2 -> 1; matrix products, arithmetic and copies ran while one was open for 52% -> 10% of each run, Pallas kernels for 0% -> 64%
where the time goes in v1:
time: 656 us; the launch traced here: 649 us
  Pallas kernels  484 us (74%)
  waiting for transfers between devices  46.5 us (7%)
  other arithmetic  38.2 us (6%)
  blocking collectives  33.6 us (5%)
  local copies, waits for them, and re-layouts  31.5 us (5%)
  between operations  14.6 us (2%)
    pallas_call x3, Pallas kernels, project(): pl.pallas_call(functools.partial(proj_kernel, epilogue, chunk), out_shape...  173 us
    pallas_call x3, Pallas kernels, add_products(): pl.pallas_call(body, out_shape=jax.ShapeDtypeStruct((rows, cols), out_dty...  170 us
    pallas_call x1, Pallas kernels, attention(): pl.pallas_call(functools.partial(attn_kernel, heads, head_dim), out_shape...  77.1 us
    pallas_call x1, Pallas kernels, keys_values(): pl.pallas_call(functools.partial(kv_kernel, half, bn, seq, chunk), out_sh...  64.8 us
    all_gather x4, waiting for transfers between devices, gather_full(): return lax.all_gather(shard, 'fsdp', axis=0, tiled=True)  46.3 us
    all_gather x1, blocking collectives, local_layer(): lax.all_gather(small, 'fsdp', axis=0, tiled=False)[:, :n_small, :own]  33.6 us
    reshape x3, local copies, waits for them, and re-layouts, local_layer(): w_up.reshape(own, n_dev, n_slabs, own).transpose(0, 2, 1, 3)  17.3 us
    convert_element_type x2, other arithmetic, layer_norm(): return (normed * gain + shift).astype(BF16)  13.9 us
  transfers between devices with their start and end apart: 4, of which 1 were waited for; matrix products, arithmetic and copies ran while one was open for 10% of the time, Pallas kernels for 64%

profile of v1, /device:TPU:97, one launch (start us, length us, event | category | flops | bytes accessed | tf_op | source)
XLA Modules:
  0.0 649.0 jit_solution(9607960048811548016)
XLA Ops:
  7.2 0.1 all-gather.6.cloned.1.call-start
  7.3 4.9 reshape.123
  12.2 0.1 all-gather.6.cloned.1.call-update
  12.2 0.1 all-gather.8.cloned.1.call-start
  12.3 8.2 %reshape.125 = bf16[80,32,4,80]{3,2,1,0:T(4,128)(2,1)} reshape(bf16[80,10240]{1,0:T(8,128)(2,1)} %param.22) | data formatting | bytes 3276800 | tf_op jit(solution)/shard_map/reshape | solution.py:224
  20.5 2.5 copy.21
  23.0 0.0 copy-start.9
  23.0 0.0 copy-start.2
  23.0 0.0 copy-start.3
  23.1 0.0 copy-start.4
  23.1 0.0 copy-start.5
  23.1 0.0 copy-start.6
  23.1 0.0 copy-start.7
  23.1 0.0 copy-start.8
  23.1 6.6 %reshape.126 = bf16[80,10240]{1,0:T(8,128)(2,1)} reshape(bf16[80,4,32,80]{3,2,1,0:T(8,128)(2,1)S(1)} %bitcast.32) | data formatting | bytes 3276800 | tf_op jit(solution)/shard_map/reshape | solution.py:224
  29.7 1.4 slice.95
  31.1 0.0 copy-done.1
  31.1 1.3 pad_maximum_fusion
  32.4 0.1 all-gather.8.cloned.1.call-update
  32.5 0.1 all-gather.10.cloned.1.call-start
  32.5 1.5 fusion.10
  34.0 0.0 slice-done.3
  34.0 1.1 pad_maximum_fusion.1
  35.1 0.1 all-gather.10.cloned.1.call-update
  35.2 0.1 all-gather.12.cloned.1.call-start
  35.3 1.0 pad_maximum_fusion.2
  36.2 0.1 all-gather.12.cloned.1.call-update
  36.3 0.1 reshape.121
  36.4 0.1 reshape.122
  36.5 0.0 copy-done.4
  36.5 0.1 concatenate.12
  36.7 33.6 %all-gather = bf16[512,128]{1,0:T(8,128)(2,1)S(1)} all-gather(bf16[16,128]{1,0:T(8,128)(2,1)S(1)} %pad.4), channel_id=2, replica_groups=mesh['dp'=1,'fsdp'=32] {'fsdp'}, dimensions={0}, use_global_device_ids=true | all-gather | bytes 135168 | tf_op jit(solution)/shard_map/all_gather | solution.py:229
  70.3 0.1 reshape.124
  70.5 0.6 slice.94.b_ref
  71.1 0.6 slice.93.b_ref
  71.7 0.1 reshape.127
  71.8 0.6 slice.100.b_ref
  72.5 0.6 slice.102.b_ref
  73.1 0.3 slice_reduce_fusion
  73.3 0.1 add.40
  73.4 0.1 mul.46
  73.5 0.7 slice.76.refs_3_
  74.2 0.1 add.44
  74.2 0.1 mul.52
  74.3 0.7 slice.88.refs_5_
  75.0 5.6 convert_reduce_fusion.1
  80.6 0.0 slice-start.2
  80.6 7.0 %fusion.7 = f32[16,128]{1,0:T(8,128)S(1)} fusion(bf16[16,128,2560]{2,1,0:T(8,128)(2,1)} %param.13, f32[16,128]{1,0:T(8,128)S(1)} %get-tuple-element.24), kind=kLoop, calls=%fused_computation.11 | loop fusion | flops 20969472 | bytes 10502144 | tf_op jit(solution)/shard_map/reduce_sum | solution.py:20
  87.6 0.0 slice-done
  87.6 0.0 slice-done.1
  87.6 7.0 %add_convert_fusion.x_ref = bf16[2048,2560]{1,0:T(8,128)(2,1)} fusion(f32[2560]{0:T(1024)S(1)} %add.40, f32[2560]{0:T(1024)S(1)} %mul.46, f32[2048]{0:T(1024)S(1)} %rsqrt_bitcast_fusion, f32[2048]{0:T(1024)S(1)} %get-tuple-element.23, bf16[16,128,2560]{2,1,0:T(8,128)(2,1)S(1)} %bitcast.31), kind=kLoop, calls=%fused_computation.12 | loop fusion | flops 31457280 | bytes 21008384 | tf_op jit(solution)/shard_map/convert_element_type | solution.py:22
  94.7 46.3 %all-gather.6.cloned.1.call-done.w_ref = bf16[2560,7680]{1,0:T(8,128)(2,1)} async-done(((bf16[80,7680]{1,0:T(8,128)(2,1)}), bf16[2560,7680]{1,0:T(8,128)(2,1)}) %all-gather.6.cloned.1.call-update) | async-done | bytes 39321616 | tf_op jit(solution)/shard_map/all_gather | solution.py:210
  140.9 34.1 %shard_map.148.q_ref = bf16[2048,2560]{1,0:T(8,128)(2,1)} custom-call(bf16[2048,2560]{1,0:T(8,128)(2,1)} %add_convert_fusion.x_ref, bf16[2560,7680]{1,0:T(8,128)(2,1)} %all-gather.6.cloned.1.call-done.w_ref, f32[1,2560]{1,0:T(1,128)} %slice.93.b_ref), custom_call_target="tpu_custom_call" | custom-call | flops 26843545600 | bytes 34078720 | tf_op jit(solution)/shard_map/pallas_call | solution.py:48
  175.1 64.8 %shard_map.149 = (bf16[16,2560,128]{2,1,0:T(8,128)(2,1)}, bf16[16,2560,128]{2,1,0:T(8,128)(2,1)}) custom-call(bf16[2048,2560]{1,0:T(8,128)(2,1)} %add_convert_fusion.x_ref, bf16[2560,7680]{1,0:T(8,128)(2,1)} %all-gather.6.cloned.1.call-done.w_ref, f32[1,5120]{1,0:T(1,128)} %slice.94.b_ref), custom_call_target="tpu_custom_call" | custom-call | flops 53687091200 | bytes 57671680 | tf_op jit(solution)/shard_map/pallas_call | solution.py:101
  239.9 77.1 %shard_map.150.refs_0_ = bf16[2048,2560]{1,0:T(8,128)(2,1)} custom-call(bf16[2048,2560]{1,0:T(8,128)(2,1)} %shard_map.148.q_ref, bf16[16,2560,128]{2,1,0:T(8,128)(2,1)} %get-tuple-element.7.k_ref, bf16[16,2560,128]{2,1,0:T(8,128)(2,1)} %get-tuple-element.8.v_ref), custom_call_target="tpu_custom_call" | custom-call | flops 12884901888 | bytes 41943040 | tf_op jit(solution)/shard_map/pallas_call | solution.py:155
  317.0 35.1 %shard_map.151.refs_4_ = bf16[2048,2560]{1,0:T(8,128)(2,1)} custom-call(bf16[2048,2560]{1,0:T(8,128)(2,1)} %shard_map.150.refs_0_, bf16[2560,10240]{1,0:T(8,128)(2,1)} %all-gather.8.cloned.1.call-done.refs_1_.w_ref, bf16[2048,2560]{1,0:T(8,128)(2,1)} %bitcast.29, f32[1,2560]{1,0:T(1,128)} %slice.76.refs_3_), custom_call_target="tpu_custom_call" | custom-call | flops 26843545600 | bytes 55050240 | tf_op jit(solution)/shard_map/pallas_call | solution.py:194
  352.1 5.6 convert_reduce_fusion
  357.7 1.4 copy-done
  359.1 2.8 fusion.2
  362.0 6.8 %fusion.5.x_ref = bf16[2048,2560]{1,0:T(8,128)(2,1)} fusion(bf16[2048,2560]{1,0:T(8,128)(2,1)S(1)} %copy-done, f32[2560]{0:T(1024)S(1)} %add.44, f32[2560]{0:T(1024)S(1)} %mul.52, f32[2048]{0:T(1024)S(1)} %add_rsqrt_fusion, f32[2048]{0:T(1024)S(1)} %broadcast_multiply_fusion), kind=kLoop, calls=%fused_computation.9 | loop fusion | flops 31457280 | bytes 21008384 | tf_op jit(solution)/shard_map/convert_element_type | solution.py:22
  368.8 101.5 %shard_map.152.refs_0_.refs_1_ = bf16[2048,7680]{1,0:T(8,128)(2,1)} custom-call(bf16[2048,2560]{1,0:T(8,128)(2,1)} %fusion.5.x_ref, bf16[2560,10240]{1,0:T(8,128)(2,1)} %all-gather.8.cloned.1.call-done.refs_1_.w_ref, f32[1,7680]{1,0:T(1,128)} %slice.100.b_ref), custom_call_target="tpu_custom_call" | custom-call | flops 80530636800 | bytes 81264640 | tf_op jit(solution)/shard_map/pallas_call | solution.py:48
  470.3 36.9 %shard_map.153.refs_1_ = bf16[2048,2560]{1,0:T(8,128)(2,1)} custom-call(bf16[2048,2560]{1,0:T(8,128)(2,1)} %fusion.5.x_ref, bf16[2560,7680]{1,0:T(8,128)(2,1)} %all-gather.10.cloned.1.call-done.w_ref.refs_2_.refs_3_, f32[1,2560]{1,0:T(1,128)} %slice.102.b_ref), custom_call_target="tpu_custom_call" | custom-call | flops 26843545600 | bytes 34078720 | tf_op jit(solution)/shard_map/pallas_call | solution.py:48
  507.2 67.7 %shard_map.154.refs_4_ = f32[2048,2560]{1,0:T(8,128)} custom-call(bf16[2048,7680]{1,0:T(8,128)(2,1)} %shard_map.152.refs_0_.refs_1_, bf16[2048,7680]{1,0:T(8,128)(2,1)} %shard_map.152.refs_0_.refs_1_, bf16[2560,7680]{1,0:T(8,128)(2,1)} %all-gather.10.cloned.1.call-done.w_ref.refs_2_.refs_3_, ...), custom_call_target="tpu_custom_call" | custom-call | flops 53687091200 | bytes 78643200 | tf_op jit(solution)/shard_map/pallas_call | solution.py:194
  574.9 67.0 %shard_map.155 = bf16[2048,2560]{1,0:T(8,128)(2,1)} custom-call(bf16[2048,7680]{1,0:T(8,128)(2,1)} %shard_map.152.refs_0_.refs_1_, bf16[2048,2560]{1,0:T(8,128)(2,1)} %shard_map.153.refs_1_, bf16[2560,5120]{1,0:T(8,128)(2,1)} %all-gather.12.cloned.1.call-done.refs_2_.refs_3_, bf16[2560,5120]{1,0:T(8,128)(2,1)} %all-gather.12.cloned.1.call-done.refs_2_.refs_3_, ...), custom_call_target="tpu_custom_call" | custom-call | flops 53687091200 | bytes 78643200 | tf_op jit(solution)/shard_map/pallas_call | solution.py:194
  (26 shorter events, 0.1 us)
Async XLA Ops:
  7.2 23.9 %copy-start.1 = (bf16[80,2560]{1,0:T(8,128)(2,1)S(1)}, bf16[80,2560]{1,0:T(8,128)(2,1)}, u32[]{:S(2)}) copy-start(bf16[80,2560]{1,0:T(8,128)(2,1)} %param.18) | copy-start | bytes 1228804
  7.2 133.8 %all-gather.6.cloned.1.call-start = ((), (), s32[]{:S(2)}) async-start(), calls=%async_computation | async-start | bytes 40550400 | tf_op jit(solution)/shard_map/all_gather | solution.py:210
  12.2 304.7 %all-gather.8.cloned.1.call-start = ((), (), s32[]{:S(2)}) async-start(), calls=%async_computation.1 | async-start | bytes 54067200 | tf_op jit(solution)/shard_map/all_gather | solution.py:210
  23.0 13.3 %copy-start.9 = (bf16[240]{0:T(256)(128)(2,1)S(1)}, bf16[240]{0:T(256)(128)(2,1)}, u32[]{:S(2)}) copy-start(bf16[240]{0:T(256)(128)(2,1)} %param.17) | copy-start | bytes 1444
  23.0 13.4 %copy-start.2 = (bf16[320]{0:T(512)(128)(2,1)S(1)}, bf16[320]{0:T(512)(128)(2,1)}, u32[]{:S(2)}) copy-start(bf16[320]{0:T(512)(128)(2,1)} %param.23) | copy-start | bytes 1924
  23.0 13.4 %copy-start.3 = (bf16[80]{0:T(256)(128)(2,1)S(1)}, bf16[80]{0:T(256)(128)(2,1)}, u32[]{:S(2)}) copy-start(bf16[80]{0:T(256)(128)(2,1)} %param.14) | copy-start | bytes 484
  23.1 13.4 %copy-start.4 = (bf16[80]{0:T(256)(128)(2,1)S(1)}, bf16[80]{0:T(256)(128)(2,1)}, u32[]{:S(2)}) copy-start(bf16[80]{0:T(256)(128)(2,1)} %param.15) | copy-start | bytes 484
  23.1 13.4 %copy-start.5 = (bf16[80]{0:T(256)(128)(2,1)S(1)}, bf16[80]{0:T(256)(128)(2,1)}, u32[]{:S(2)}) copy-start(bf16[80]{0:T(256)(128)(2,1)} %param.19) | copy-start | bytes 484
  23.1 13.4 %copy-start.6 = (bf16[80]{0:T(256)(128)(2,1)S(1)}, bf16[80]{0:T(256)(128)(2,1)}, u32[]{:S(2)}) copy-start(bf16[80]{0:T(256)(128)(2,1)} %param.20) | copy-start | bytes 484
  23.1 13.4 %copy-start.7 = (bf16[80]{0:T(256)(128)(2,1)S(1)}, bf16[80]{0:T(256)(128)(2,1)}, u32[]{:S(2)}) copy-start(bf16[80]{0:T(256)(128)(2,1)} %param.21) | copy-start | bytes 484
  23.1 13.4 %copy-start.8 = (bf16[80]{0:T(256)(128)(2,1)S(1)}, bf16[80]{0:T(256)(128)(2,1)}, u32[]{:S(2)}) copy-start(bf16[80]{0:T(256)(128)(2,1)} %param.25) | copy-start | bytes 484
  29.7 4.4 slice-start.3
  32.5 437.8 %all-gather.10.cloned.1.call-start = ((), (), s32[]{:S(2)}) async-start(), calls=%async_computation.2 | async-start | bytes 40550400 | tf_op jit(solution)/shard_map/all_gather | solution.py:210
  35.2 539.7 %all-gather.12.cloned.1.call-start = ((), (), s32[]{:S(2)}) async-start(), calls=%async_computation.3 | async-start | bytes 27033600 | tf_op jit(solution)/shard_map/all_gather | solution.py:210
  75.0 12.6 %slice-start = ((s8[10485760]{0:T(1024)(128)(4,1)}), s8[4194304]{0:T(1024)(128)(4,1)S(1)}, s32[]{:S(2)}) async-start(s8[10485760]{0:T(1024)(128)(4,1)} %bitcast.30), calls=%async_computation.4 | async-start | bytes 8388608
  75.0 12.6 %slice-start.1 = ((s8[10485760]{0:T(1024)(128)(4,1)}), s8[4194304]{0:T(1024)(128)(4,1)S(1)}, s32[]{:S(2)}) async-start(s8[10485760]{0:T(1024)(128)(4,1)} %bitcast.30), calls=%async_computation.5 | async-start | bytes 8388608
  80.6 7.0 %slice-start.2 = ((s8[10485760]{0:T(1024)(128)(4,1)}), s8[2097152]{0:T(1024)(128)(4,1)S(1)}, s32[]{:S(2)}) async-start(s8[10485760]{0:T(1024)(128)(4,1)} %bitcast.30), calls=%async_computation.6 | async-start | bytes 4194304
  352.1 7.0 %copy-start = (bf16[2048,2560]{1,0:T(8,128)(2,1)S(1)}, bf16[2048,2560]{1,0:T(8,128)(2,1)}, u32[]{:S(2)}) copy-start(bf16[2048,2560]{1,0:T(8,128)(2,1)} %shard_map.151.refs_4_) | copy-start | bytes 31457284
Sparse Core Ops, SparseCore 0:
  12.4 128.5 all-gather.5
  143.0 156.8 all-gather.7
  302.0 122.5 all-gather.9
  426.5 88.4 all-gather.11

commit v2 on v1

--- a/solution.py
+++ b/solution.py
@@ -50,7 +50,7 @@
         out_shape=jax.ShapeDtypeStruct((rows, n_cols), BF16),
         grid=(rows // bm, n_cols // bn),
         in_specs=[
-            pl.BlockSpec((bm, k), lambda m, n: (m, 0)),
+            pl.BlockSpec((bm, k), lambda m, n: (m, 0), pipeline_mode=pl.Buffered(1 if bm == rows else 2)),
             pl.BlockSpec((k, bn), lambda m, n: (0, n + off)),
             pl.BlockSpec((1, bn), lambda m, n: (0, n)),
         ],
@@ -60,58 +60,102 @@
     )(x, w, bias)
 
 
-def kv_kernel(half, bn, seq, chunk, x_ref, w_ref, b_ref, k_hbm, v_hbm, buf, sem):
+def qkv_kernel(part, bn, seq, chunk, x_ref, w_ref, b_ref, q_hbm, k_hbm, v_hbm, flat, buf, flat_sem, sem):
     n = pl.program_id(0)
-    total = 2 * half
     slot = lax.rem(n, 2)
 
-    def copy(dst, col_block, which):
-        cols = pl.ds(pl.multiple_of(col_block * bn, bn), bn)
+    def flat_copy(block, which):
+        cols = pl.ds(pl.multiple_of(block * bn, bn), bn)
+        return pltpu.make_async_copy(flat.at[which], q_hbm.at[:, cols], flat_sem.at[which])
+
+    def copy(dst, block, which):
+        cols = pl.ds(pl.multiple_of(block * bn, bn), bn)
         return pltpu.make_async_copy(buf.at[which], dst.at[:, cols, :], sem.at[which])
 
-    @pl.when(n >= 2)
+    def product(start, size):
+        acc = jnp.dot(x_ref[start:start + size, :], w_ref[...], preferred_element_type=F32)
+        return (acc + b_ref[...]).astype(BF16)
+
+    @pl.when((n >= 2) & (n < part + 2))
+    def _():
+        flat_copy(0, slot).wait()
+
+    @pl.when(n >= part + 2)
     def _():
         copy(k_hbm, 0, slot).wait()
 
-    for start, size in row_chunks(x_ref.shape[0], chunk):
-        acc = jnp.dot(x_ref[start:start + size, :], w_ref[...], preferred_element_type=F32)
-        turned = (acc + b_ref[...]).astype(BF16).T
-        for i in range(size // seq):
-            buf[slot, start // seq + i] = turned[:, i * seq:(i + 1) * seq]
-
-    @pl.when(n < half)
-    def _():
-        copy(k_hbm, n, slot).start()
-
-    @pl.when(n >= half)
-    def _():
-        copy(v_hbm, n - half, slot).start()
-
-    @pl.when(n == total - 1)
+    @pl.when(n < part)
+    def _():
+        for start, size in row_chunks(x_ref.shape[0], chunk):
+            flat[slot, start:start + size, :] = product(start, size)
+        flat_copy(n, slot).start()
+
+    @pl.when(n >= part)
+    def _():
+        for start, size in row_chunks(x_ref.shape[0], chunk):
+            turned = product(start, size).T
+            for i in range(size // seq):
+                buf[slot, start // seq + i] = turned[:, i * seq:(i + 1) * seq]
+
+    @pl.when((n >= part) & (n < 2 * part))
+    def _():
+        copy(k_hbm, n - part, slot).start()
+
+    @pl.when(n >= 2 * part)
+    def _():
+        copy(v_hbm, n - 2 * part, slot).start()
+
+    @pl.when(n == 3 * part - 1)
     def _():
         copy(v_hbm, 0, 1 - slot).wait()
         copy(v_hbm, 0, slot).wait()
 
 
-def keys_values(x, w, first_col, width, bias, seq, bn=256, chunk=256):
+def queries_keys_values(x, w, width, bias, seq, bn=256, chunk=256):
     rows, k = x.shape
     batch = rows // seq
-    off, half = first_col // bn, width // bn
-    shape = jax.ShapeDtypeStruct((batch, width, seq), BF16)
-    return pl.pallas_call(
-        functools.partial(kv_kernel, half, bn, seq, chunk),
-        out_shape=(shape, shape),
-        grid=(2 * half,),
+    part = width // bn
+    turned = jax.ShapeDtypeStruct((batch, width, seq), BF16)
+    anywhere = pl.BlockSpec(memory_space=pl.ANY)
+    return pl.pallas_call(
+        functools.partial(qkv_kernel, part, bn, seq, chunk),
+        out_shape=(jax.ShapeDtypeStruct((rows, width), BF16), turned, turned),
+        grid=(3 * part,),
         in_specs=[
             pl.BlockSpec((rows, k), lambda n: (0, 0), pipeline_mode=pl.Buffered(1)),
-            pl.BlockSpec((k, bn), lambda n: (0, n + off)),
+            pl.BlockSpec((k, bn), lambda n: (0, n)),
             pl.BlockSpec((1, bn), lambda n: (0, n)),
         ],
-        out_specs=(pl.BlockSpec(memory_space=pl.ANY), pl.BlockSpec(memory_space=pl.ANY)),
-        scratch_shapes=[pltpu.VMEM((2, batch, bn, seq), BF16), pltpu.SemaphoreType.DMA((2,))],
+        out_specs=(anywhere, anywhere, anywhere),
+        scratch_shapes=[
+            pltpu.VMEM((2, rows, bn), BF16),
+            pltpu.VMEM((2, batch, bn, seq), BF16),
+            pltpu.SemaphoreType.DMA((2,)),
+            pltpu.SemaphoreType.DMA((2,)),
+        ],
         compiler_params=params(58, 1),
-        cost_estimate=cost(4 * rows * k * width, 2 * (rows * k + 2 * k * width + 2 * rows * width)),
+        cost_estimate=cost(6 * rows * k * width, 2 * (rows * k + 3 * k * width + 3 * rows * width)),
     )(x, w, bias)
+
+
+def norm_kernel(chunk, x_ref, g_ref, s_ref, o_ref):
+    for start, size in row_chunks(x_ref.shape[0], chunk):
+        o_ref[start:start + size, :] = layer_norm(x_ref[start:start + size, :], g_ref[...], s_ref[...])
+
+
+def norm_rows(x, gain, shift, bm=256, chunk=16):
+    rows, d = x.shape
+    block = pl.BlockSpec((bm, d), lambda m: (m, 0))
+    vector = pl.BlockSpec((1, d), lambda m: (0, 0))
+    return pl.pallas_call(
+        functools.partial(norm_kernel, chunk),
+        out_shape=jax.ShapeDtypeStruct((rows, d), BF16),
+        grid=(rows // bm,),
+        in_specs=[block, vector, vector],
+        out_specs=block,
+        compiler_params=params(32, 1),
+        cost_estimate=cost(10 * rows * d, 4 * rows * d),
+    )(x, gain, shift)
 
 
 def attn_kernel(heads, head_dim, q_ref, k_ref, v_ref, o_ref):
@@ -121,12 +165,14 @@
     key = lax.broadcasted_iota(jnp.int32, (seq, seq), 1)
     allowed = key <= query
     columns = {}
-    for h in range(heads):
-        lo, hi = h * head_dim, (h + 1) * head_dim
-        base = lo // LANES * LANES
-        width = pl.cdiv(hi - base, LANES) * LANES
-
-        def padded(ref):
+    group = 2
+    for first in range(0, heads, group):
+        members = [(h * head_dim, (h + 1) * head_dim) for h in range(first, first + group)]
+        base = members[0][0] // LANES * LANES
+        last = members[-1][1]
+        width = pl.cdiv(last - base, LANES) * LANES
+
+        def window(ref, lo, hi):
             parts = [ref[0, lo:hi, :]]
             if lo > base:
                 parts.insert(0, jnp.zeros((lo - base, seq), BF16))
@@ -134,17 +180,23 @@
                 parts.append(jnp.zeros((base + width - hi, seq), BF16))
             return jnp.concatenate(parts, axis=0) if len(parts) > 1 else parts[0]
 
-        scores = jnp.dot(q_ref[:, base:base + width], padded(k_ref), preferred_element_type=F32) * scale
-        scores = jnp.where(allowed, scores, -jnp.inf)
-        peak = jnp.max(scores, axis=-1, keepdims=True)
-        weights = jnp.exp(scores - peak)
-        probs = (weights * (1.0 / jnp.sum(weights, axis=-1, keepdims=True))).astype(BF16)
-        part = lax.dot_general(probs, padded(v_ref), (((1,), (1,)), ((), ())), preferred_element_type=F32)
+        def side_by_side(ref):
+            return jnp.concatenate([window(ref, lo, hi) for lo, hi in members], axis=1)
+
+        both = jnp.dot(q_ref[:, base:base + width], side_by_side(k_ref), preferred_element_type=F32)
+        probs = []
+        for i in range(group):
+            scores = jnp.where(allowed, both[:, i * seq:(i + 1) * seq] * scale, -jnp.inf)
+            peak = jnp.max(scores, axis=-1, keepdims=True)
+            weights = jnp.exp(scores - peak)
+            probs.append((weights * (1.0 / jnp.sum(weights, axis=-1, keepdims=True))).astype(BF16))
+        part = lax.dot_general(
+            jnp.concatenate(probs, axis=1), side_by_side(v_ref), (((1,), (1,)), ((), ())), preferred_element_type=F32)
         for i in range(width // LANES):
             col = base // LANES + i
             piece = part[:, i * LANES:(i + 1) * LANES]
             columns[col] = columns[col] + piece if col in columns else piece
-        for col in [c for c in columns if (c + 1) * LANES <= hi]:
+        for col in [c for c in columns if (c + 1) * LANES <= last]:
             o_ref[:, col * LANES:(col + 1) * LANES] = columns.pop(col).astype(BF16)
 
 
@@ -233,21 +285,19 @@
 
         bqkv = vectors[:, 6:9].reshape(1, 3 * width)
         vectors = vectors.transpose(1, 0, 2).reshape(n_small, d)
-        g1, s1, bo, g2, s2, bd = vectors[0], vectors[1], vectors[2:3], vectors[3], vectors[4], vectors[5:6]
+        g1, s1, bo, g2, s2, bd = [vectors[i:i + 1] for i in range(6)]
         bup = vectors[9:].reshape(1, n_slabs * d)
 
         x = prompts.reshape(rows, d)
-        normed1 = layer_norm(x, g1, s1)
-        identity = lambda t: t
+        normed1 = norm_rows(x, g1, s1)
         gelu = functools.partial(jax.nn.gelu, approximate=True)
-        k_t, v_t = keys_values(normed1, full_a, width, width, bqkv[:, width:], seq)
-        q = project(normed1, full_a, 0, width, bqkv[:, :width], identity, rows // 2, 512)
+        q, k_t, v_t = queries_keys_values(normed1, full_a, width, bqkv, seq)
         ctx = attention(q, k_t, v_t, heads, head_dim)
-        x1 = add_products([(ctx, 0, full_b, 0)], x, bo, BF16, rows // 2, 512)
-        normed2 = layer_norm(x1, g2, s2)
-        hid_a = project(normed2, full_b, width, cut, bup[:, :cut], gelu, rows // 2, 512)
+        x1 = add_products([(ctx, 0, full_b, 0)], x, bo, BF16, rows, 256)
+        normed2 = norm_rows(x1, g2, s2)
+        hid_a = project(normed2, full_b, width, cut, bup[:, :cut], gelu, rows, 256)
         normed2, hid_a = lax.optimization_barrier((normed2, hid_a))
-        hid_b = project(normed2, full_c, 0, d, bup[:, cut:], gelu, rows // 2, 512)
+        hid_b = project(normed2, full_c, 0, d, bup[:, cut:], gelu, rows, 256)
         part = add_products([(hid_a, 0, full_c, d), (hid_a, d, full_c, 2 * d)], x1, bd, F32, rows // 2, 256)
         y = add_products([(hid_a, 2 * d, full_d, 0), (hid_b, 0, full_d, d)], part, None, BF16, rows // 2, 256)
 

time: 656 us -> 630 us (0.960); the launches traced: 649 us -> 630 us
  other arithmetic: 38.2 us -> 3.45 us
  waiting for transfers between devices: 46.5 us -> 71.3 us
  Pallas kernels: 484 us -> 467 us
  local copies, waits for them, and re-layouts: 31.5 us -> 41.4 us
    pallas_call x1 -> x3, Pallas kernels: 64.8 us -> 109 us  [the longest x1 94.1 us: queries_keys_values(): pl.pallas_call(functools.partial(qkv_kernel, part, bn, seq, chunk), out_s...]
    pallas_call x3 -> x2, Pallas kernels: 173 us -> 138 us  [project(): pl.pallas_call(functools.partial(proj_kernel, epilogue, chunk), out_shape...]
    pallas_call x1, Pallas kernels: 77.1 us -> 49.3 us  [attention(): pl.pallas_call(functools.partial(attn_kernel, heads, head_dim), out_shape...]
    all_gather x4, waiting for transfers between devices: 46.3 us -> 71.1 us  [gather_full(): return lax.all_gather(shard, 'fsdp', axis=0, tiled=True)]
    reduce_sum x4 -> x0, other arithmetic: 21 us -> none  [the longest x2 11.1 us: layer_norm(): mean_val = jnp.mean(act_f32, axis=-1, keepdims=True)]
    unnamed x26 -> x30, local copies, waits for them, and re-layouts: 1.45 us -> 16.7 us
    convert_element_type x2 -> x0, other arithmetic: 13.9 us -> none  [layer_norm(): return (normed * gain + shift).astype(BF16)]
  transfers between devices with their start and end apart: 4 -> 4, of which waited for: 1 -> 2; matrix products, arithmetic and copies ran while one was open for 10% -> 3% of each run, Pallas kernels for 64% -> 63%
where the time goes in v2:
time: 630 us
  Pallas kernels  467 us (74%)
  waiting for transfers between devices  71.3 us (11%)
  local copies, waits for them, and re-layouts  41.4 us (7%)
  blocking collectives  33.1 us (5%)
  between operations  14 us (2%)
    pallas_call x3, Pallas kernels, add_products(): pl.pallas_call(body, out_shape=jax.ShapeDtypeStruct((rows, cols), out_dty...  170 us
    pallas_call x2, Pallas kernels, project(): pl.pallas_call(functools.partial(proj_kernel, epilogue, chunk), out_shape...  138 us
    pallas_call x1, Pallas kernels, queries_keys_values(): pl.pallas_call(functools.partial(qkv_kernel, part, bn, seq, chunk), out_s...  94.1 us
    all_gather x4, waiting for transfers between devices, gather_full(): return lax.all_gather(shard, 'fsdp', axis=0, tiled=True)  71.1 us
    pallas_call x1, Pallas kernels, attention(): pl.pallas_call(functools.partial(attn_kernel, heads, head_dim), out_shape...  49.3 us
    all_gather x1, blocking collectives, local_layer(): lax.all_gather(small, 'fsdp', axis=0, tiled=False)[:, :n_small, :own]  33.1 us
    unnamed x30, local copies, waits for them, and re-layouts  16.7 us
    pallas_call x2, Pallas kernels, norm_rows(): pl.pallas_call(functools.partial(norm_kernel, chunk), out_shape=jax.Shape...  15.4 us
  transfers between devices with their start and end apart: 4, of which 2 were waited for; matrix products, arithmetic and copies ran while one was open for 3% of the time, Pallas kernels for 63%

profile of v2, /device:TPU:97, one launch (start us, length us, event | category | flops | bytes accessed | tf_op | source)
XLA Modules:
  0.0 630.1 jit_solution(15510655763147499873)
XLA Ops:
  7.2 0.0 copy-start.5
  7.2 0.1 all-gather.6.cloned.1.call-start
  7.3 5.0 reshape.75
  12.2 0.1 all-gather.6.cloned.1.call-update
  12.3 0.1 all-gather.8.cloned.1.call-start
  12.4 0.0 copy-done.5
  12.4 4.4 reshape.77
  16.8 2.5 copy.21
  19.3 0.0 copy-start.6
  19.3 6.6 %reshape.78 = bf16[80,10240]{1,0:T(8,128)(2,1)} reshape(bf16[80,4,32,80]{3,2,1,0:T(8,128)(2,1)S(1)} %bitcast.26) | data formatting | bytes 3276800 | tf_op jit(solution)/shard_map/reshape | solution.py:276
  25.9 0.0 copy-done.6
  25.9 1.3 slice-done
  27.2 1.3 pad_maximum_fusion
  28.5 0.1 all-gather.8.cloned.1.call-update
  28.5 0.0 slice-start.1
  28.6 0.1 all-gather.10.cloned.1.call-start
  28.6 0.6 copy-done.4
  29.2 0.1 fusion.1
  29.3 0.3 slice-done.1
  29.7 1.1 pad_maximum_fusion.1
  30.8 0.0 copy-start.10
  30.8 0.0 copy-start.11
  30.8 0.0 copy-start.12
  30.8 0.0 copy-start.13
  30.9 0.1 all-gather.10.cloned.1.call-update
  30.9 0.1 all-gather.12.cloned.1.call-start
  31.0 1.0 pad_maximum_fusion.2
  32.0 0.1 all-gather.12.cloned.1.call-update
  32.1 0.0 copy-done.14
  32.1 0.1 reshape.73
  32.1 0.0 copy-done.7
  32.2 0.1 reshape.74
  32.2 0.0 copy-done.8
  32.2 0.0 copy-done.9
  32.3 0.1 concatenate.12
  32.4 33.1 %all-gather = bf16[512,128]{1,0:T(8,128)(2,1)S(1)} all-gather(bf16[16,128]{1,0:T(8,128)(2,1)S(1)} %pad.4), channel_id=2, replica_groups=mesh['dp'=1,'fsdp'=32] {'fsdp'}, dimensions={0}, use_global_device_ids=true | all-gather | bytes 135168 | tf_op jit(solution)/shard_map/all_gather | solution.py:281
  65.6 0.1 reshape.79
  65.7 0.6 slice.102.b_ref
  66.3 0.6 slice.104.b_ref
  66.9 0.3 slice_reduce_fusion
  67.2 0.1 slice.72.g_ref
  67.3 0.1 slice.74.s_ref
  67.4 0.7 reshape.76.b_ref
  68.2 0.7 slice.78.refs_3_
  68.8 0.1 slice.80.g_ref
  68.9 0.1 slice.82.s_ref
  69.0 0.7 slice.92.refs_5_
  69.7 4.0 copy-done
  73.7 7.7 %shard_map.148.x_ref = bf16[2048,2560]{1,0:T(8,128)(2,1)S(1)} custom-call(bf16[2048,2560]{1,0:T(8,128)(2,1)S(1)} %bitcast.25, f32[1,2560]{1,0:T(1,128)S(1)} %slice.72.g_ref, f32[1,2560]{1,0:T(1,128)S(1)} %slice.74.s_ref), custom_call_target="tpu_custom_call" | custom-call | flops 52428800 | bytes 20971520 | tf_op jit(solution)/shard_map/pallas_call | solution.py:150
  81.4 0.0 copy-start.2
  81.4 4.1 copy-done.2
  85.5 55.5 %all-gather.6.cloned.1.call-done.w_ref = bf16[2560,7680]{1,0:T(8,128)(2,1)} async-done(((bf16[80,7680]{1,0:T(8,128)(2,1)}), bf16[2560,7680]{1,0:T(8,128)(2,1)}) %all-gather.6.cloned.1.call-update) | async-done | bytes 39321616 | tf_op jit(solution)/shard_map/all_gather | solution.py:262
  141.0 94.1 %shard_map.149 = (bf16[2048,2560]{1,0:T(8,128)(2,1)}, bf16[16,2560,128]{2,1,0:T(8,128)(2,1)}, bf16[16,2560,128]{2,1,0:T(8,128)(2,1)}) custom-call(bf16[2048,2560]{1,0:T(8,128)(2,1)} %copy-done.2, bf16[2560,7680]{1,0:T(8,128)(2,1)} %all-gather.6.cloned.1.call-done.w_ref, f32[1,7680]{1,0:T(1,128)} %reshape.76.b_ref), custom_call_target="tpu_custom_call" | custom-call | flops 80530636800 | bytes 81264640 | tf_op jit(solution)/shard_map/pallas_call | solution.py:120
  235.0 49.3 %shard_map.150.refs_0_ = bf16[2048,2560]{1,0:T(8,128)(2,1)} custom-call(bf16[2048,2560]{1,0:T(8,128)(2,1)} %get-tuple-element.8.q_ref, bf16[16,2560,128]{2,1,0:T(8,128)(2,1)} %get-tuple-element.9.k_ref, bf16[16,2560,128]{2,1,0:T(8,128)(2,1)} %get-tuple-element.10.v_ref), custom_call_target="tpu_custom_call" | custom-call | flops 12884901888 | bytes 41943040 | tf_op jit(solution)/shard_map/pallas_call | solution.py:207
  284.3 15.6 %all-gather.8.cloned.1.call-done.refs_1_.w_ref = bf16[2560,10240]{1,0:T(8,128)(2,1)} async-done(((bf16[80,10240]{1,0:T(8,128)(2,1)}), bf16[2560,10240]{1,0:T(8,128)(2,1)}) %all-gather.8.cloned.1.call-update) | async-done | bytes 52428816 | tf_op jit(solution)/shard_map/all_gather | solution.py:262
  299.9 35.1 %shard_map.151.x_ref.refs_4_ = bf16[2048,2560]{1,0:T(8,128)(2,1)} custom-call(bf16[2048,2560]{1,0:T(8,128)(2,1)} %shard_map.150.refs_0_, bf16[2560,10240]{1,0:T(8,128)(2,1)} %all-gather.8.cloned.1.call-done.refs_1_.w_ref, bf16[2048,2560]{1,0:T(8,128)(2,1)} %bitcast.24, f32[1,2560]{1,0:T(1,128)} %slice.78.refs_3_), custom_call_target="tpu_custom_call" | custom-call | flops 26843545600 | bytes 55050240 | tf_op jit(solution)/shard_map/pallas_call | solution.py:246
  335.0 4.0 copy-done.1
  339.0 7.7 %shard_map.152.x_ref = bf16[2048,2560]{1,0:T(8,128)(2,1)S(1)} custom-call(bf16[2048,2560]{1,0:T(8,128)(2,1)S(1)} %copy-done.1, f32[1,2560]{1,0:T(1,128)S(1)} %slice.80.g_ref, f32[1,2560]{1,0:T(1,128)S(1)} %slice.82.s_ref), custom_call_target="tpu_custom_call" | custom-call | flops 52428800 | bytes 20971520 | tf_op jit(solution)/shard_map/pallas_call | solution.py:150
  346.6 0.0 copy-start.3
  346.6 4.1 copy-done.3
  350.7 101.0 %shard_map.153.refs_0_.refs_1_ = bf16[2048,7680]{1,0:T(8,128)(2,1)} custom-call(bf16[2048,2560]{1,0:T(8,128)(2,1)} %copy-done.3, bf16[2560,10240]{1,0:T(8,128)(2,1)} %all-gather.8.cloned.1.call-done.refs_1_.w_ref, f32[1,7680]{1,0:T(1,128)} %slice.102.b_ref), custom_call_target="tpu_custom_call" | custom-call | flops 80530636800 | bytes 81264640 | tf_op jit(solution)/shard_map/pallas_call | solution.py:48
  451.7 37.3 %shard_map.154.refs_1_ = bf16[2048,2560]{1,0:T(8,128)(2,1)} custom-call(bf16[2048,2560]{1,0:T(8,128)(2,1)} %copy-done.3, bf16[2560,7680]{1,0:T(8,128)(2,1)} %all-gather.10.cloned.1.call-done.w_ref.refs_2_.refs_3_, f32[1,2560]{1,0:T(1,128)} %slice.104.b_ref), custom_call_target="tpu_custom_call" | custom-call | flops 26843545600 | bytes 34078720 | tf_op jit(solution)/shard_map/pallas_call | solution.py:48
  489.0 67.5 %shard_map.155.refs_4_ = f32[2048,2560]{1,0:T(8,128)} custom-call(bf16[2048,7680]{1,0:T(8,128)(2,1)} %shard_map.153.refs_0_.refs_1_, bf16[2048,7680]{1,0:T(8,128)(2,1)} %shard_map.153.refs_0_.refs_1_, bf16[2560,7680]{1,0:T(8,128)(2,1)} %all-gather.10.cloned.1.call-done.w_ref.refs_2_.refs_3_, ...), custom_call_target="tpu_custom_call" | custom-call | flops 53687091200 | bytes 78643200 | tf_op jit(solution)/shard_map/pallas_call | solution.py:246
  556.6 67.0 %shard_map.156 = bf16[2048,2560]{1,0:T(8,128)(2,1)} custom-call(bf16[2048,7680]{1,0:T(8,128)(2,1)} %shard_map.153.refs_0_.refs_1_, bf16[2048,2560]{1,0:T(8,128)(2,1)} %shard_map.154.refs_1_, bf16[2560,5120]{1,0:T(8,128)(2,1)} %all-gather.12.cloned.1.call-done.refs_2_.refs_3_, bf16[2560,5120]{1,0:T(8,128)(2,1)} %all-gather.12.cloned.1.call-done.refs_2_.refs_3_, ...), custom_call_target="tpu_custom_call" | custom-call | flops 53687091200 | bytes 78643200 | tf_op jit(solution)/shard_map/pallas_call | solution.py:246
  (19 shorter events, 0.1 us)
Async XLA Ops:
  7.2 5.2 copy-start.5
  7.2 133.8 %all-gather.6.cloned.1.call-start = ((), (), s32[]{:S(2)}) async-start(), calls=%async_computation | async-start | bytes 40550400 | tf_op jit(solution)/shard_map/all_gather | solution.py:262
  12.3 287.6 %all-gather.8.cloned.1.call-start = ((), (), s32[]{:S(2)}) async-start(), calls=%async_computation.1 | async-start | bytes 54067200 | tf_op jit(solution)/shard_map/all_gather | solution.py:262
  19.3 6.6 %copy-start.6 = (bf16[80,2560]{1,0:T(8,128)(2,1)S(1)}, bf16[80,2560]{1,0:T(8,128)(2,1)}, u32[]{:S(2)}) copy-start(bf16[80,2560]{1,0:T(8,128)(2,1)} %param.18) | copy-start | bytes 1228804
  25.9 1.3 slice-start
  27.2 2.0 copy-start.4
  28.5 1.1 slice-start.1
  28.6 423.2 %all-gather.10.cloned.1.call-start = ((), (), s32[]{:S(2)}) async-start(), calls=%async_computation.2 | async-start | bytes 40550400 | tf_op jit(solution)/shard_map/all_gather | solution.py:262
  30.8 1.3 copy-start.14
  30.8 1.4 copy-start.7
  30.8 1.4 copy-start.8
  30.8 1.4 copy-start.9
  30.8 1.4 copy-start.10
  30.8 1.4 copy-start.11
  30.8 1.4 copy-start.12
  30.8 1.4 copy-start.13
  30.9 525.6 %all-gather.12.cloned.1.call-start = ((), (), s32[]{:S(2)}) async-start(), calls=%async_computation.3 | async-start | bytes 27033600 | tf_op jit(solution)/shard_map/all_gather | solution.py:262
  69.7 4.0 copy-start
  81.4 4.1 copy-start.2
  335.0 4.0 copy-start.1
  346.6 4.1 copy-start.3
Sparse Core Ops, SparseCore 0:
  12.4 128.4 all-gather.5
  143.0 156.8 all-gather.7
  302.0 122.5 all-gather.9
  426.5 88.4 all-gather.11
